TPU v7x, 32 devices: a whole 2x2x4 slice. The times are simulated.
32 devices in a mesh: rep: 1, r: 8 (over y, z), s: 4 (over x, core).
Axes of the slice: x: 2, y: 2, z: 4, core: 2. Of those that a mesh axis runs over, the one named last changes fastest.
Arguments:
- x: bfloat16 [32, 4096, 640], P(('rep', 'r', 's'))
- dy: bfloat16 [32, 4096, 640], P(('rep', 'r', 's'))
- w_gate: bfloat16 [2, 640, 2048], P(None, 's')
- w_up: bfloat16 [2, 640, 2048], P(None, 's')
- w_down: bfloat16 [2, 2048, 640], P(None, 's')
- m_w_gate: float32 [2, 640, 2048], P(None, 's')
- m_w_up: float32 [2, 640, 2048], P(None, 's')
- m_w_down: float32 [2, 2048, 640], P(None, 's')
- v_w_gate: float32 [2, 640, 2048], P(None, 's')
- v_w_up: float32 [2, 640, 2048], P(None, 's')
- v_w_down: float32 [2, 2048, 640], P(None, 's')
Outputs:
- output 1: bfloat16 [2, 640, 2048], P('rep', 's')
- output 2: bfloat16 [2, 640, 2048], P('rep', 's')
- output 3: bfloat16 [2, 2048, 640], P('rep', 's')
- output 4: float32 [2, 640, 2048], P('rep', 's')
- output 5: float32 [2, 640, 2048], P('rep', 's')
- output 6: float32 [2, 2048, 640], P('rep', 's')
- output 7: float32 [2, 640, 2048], P('rep', 's')
- output 8: float32 [2, 640, 2048], P('rep', 's')
- output 9: float32 [2, 2048, 640], P('rep', 's')
All inputs are finite; a program needn't handle non-finite values.
Results may differ from a plain program's by a relative error of at most 0.022.
Values are sent between devices in bfloat16 or wider.
A program may use at most 2 GiB of HBM per device.

v0:
```python
import jax
import jax.numpy as jnp
from jax import lax
from jax.sharding import PartitionSpec as P

NAMES = ("w_gate", "w_up", "w_down")


def matmul(a, w):
    return jnp.dot(a, w, preferred_element_type=jnp.float32).astype(jnp.bfloat16)


def normed(h):
    wide = h.astype(jnp.float32)
    scale = lax.rsqrt(jnp.mean(wide**2, -1, keepdims=True) + 1e-6)
    return (wide * scale).astype(jnp.bfloat16)


def layer(h, w):
    a = normed(h)
    gate = jnp.dot(a, w["w_gate"], preferred_element_type=jnp.float32)
    up = jnp.dot(a, w["w_up"], preferred_element_type=jnp.float32)
    return h + matmul((jax.nn.silu(gate) * up).astype(jnp.bfloat16), w["w_down"])


def adamw(w, m, v, g):
    m = 0.9 * m + 0.1 * g
    v = 0.95 * v + 0.05 * g * g
    step = m * lax.rsqrt(v + 1e-8) + 0.1 * w
    return (w - 0.02 * step).astype(jnp.bfloat16), m, v


def clipped(gradients, sum_of_squares, count):
    factor = jnp.minimum(1.0, 0.5 * lax.rsqrt(sum_of_squares / count + 1e-30))
    return [g * factor for g in gradients]


def solution(mesh):
    def fetched(weights, number):
        return {name: lax.all_gather(w[number], "s", axis=0, tiled=True) for name, w in zip(NAMES, weights, strict=True)}

    def summed(term):
        return lax.psum(lax.psum_scatter(term, "s", scatter_dimension=0, tiled=True), "r")

    def step(x, dy, *arrays):
        weights, m, v = (arrays[i : i + 3] for i in (0, 3, 6))
        layers = weights[0].shape[0]
        h, kept = x[0], []
        for number in range(layers):
            kept.append(h)
            h = layer(h, fetched(weights, number))
        by_h, mine = dy[0], [None] * layers
        for number in reversed(range(layers)):
            _, back = jax.vjp(lambda w, h: layer(h, w), fetched(weights, number), kept[number])
            by_w, by_h = back(by_h)
            mine[number] = [summed(by_w[name]) for name in NAMES]
        gradients = [jnp.stack([mine[number][i] for number in range(layers)]).astype(jnp.float32) for i in range(3)]
        squares = lax.psum(sum(jnp.sum(g * g) for g in gradients), "s")
        gradients = clipped(gradients, squares, lax.psum(1, "s") * sum(g.size for g in gradients))
        new = [adamw(w.astype(jnp.float32), m, v, g) for w, m, v, g in zip(weights, m, v, gradients, strict=True)]
        return tuple(one[which] for which in range(3) for one in new)

    states, cut = P(("rep", "r", "s"), None, None), P(None, "s", None)
    return jax.shard_map(
        step,
        mesh=mesh,
        in_specs=(states, states) + (cut,) * 9,
        out_specs=(P("rep", "s", None),) * 9,
        check_vma=False,
    )
```

profile of v0, /device:TPU:0, one launch (start us, length us, event | category | flops | bytes accessed | tf_op | source)
XLA Modules:
  0.0 707.4 jit_solution(7181220150134081485)
XLA Ops:
  7.2 0.0 all-gather.13.cloned.1.call-start
  7.2 2.6 fusion.103
  9.8 0.0 all-gather.13.cloned.1.call-update
  9.8 0.0 all-gather.15.cloned.1.call-start
  9.9 2.5 fusion.102
  12.4 0.0 all-gather.15.cloned.1.call-update
  12.4 0.0 all-gather.17.cloned.1.call-start
  12.5 1.2 fusion.101
  13.7 0.0 all-gather.21.cloned.1.call-start
  13.7 0.5 all-gather.21.cloned.1.call-update
  14.2 0.0 all-gather.23.cloned.1.call-start
  14.3 0.5 all-gather.23.cloned.1.call-update
  14.8 0.0 all-gather.19.cloned.1.call-start
  14.9 0.5 all-gather.19.cloned.1.call-update
  15.4 0.0 reduce-scatter.15.cloned.1.call-start
  15.4 7.9 %copy.20 = bf16[1,4096,640]{1,2,0:T(8,128)(2,1)} copy(bf16[1,4096,640]{2,1,0:T(8,128)(2,1)} %param.11) | data formatting | bytes 10485760 | tf_op args[0]
  23.4 3.6 fusion.15
  27.0 8.0 %copy.21 = bf16[1,4096,640]{1,2,0:T(8,128)(2,1)} copy(bf16[1,4096,640]{2,1,0:T(8,128)(2,1)} %param.12) | data formatting | bytes 10485760 | tf_op args[1]
  35.0 3.1 all-gather.13.cloned.1.call-done
  38.1 21.8 %fusion.40 = f32[4096,2048]{1,0:T(8,128)} fusion(bf16[1,4096,640]{1,2,0:T(8,128)(2,1)} %copy.20, f32[4096]{0:T(1024)S(1)} %add_rsqrt_fusion, bf16[1,640,2048]{2,1,0:T(8,128)(2,1)} %all-gather.13.cloned.1.call-done), kind=kOutput, calls=%fused_computation.55 | convolution fusion | flops 10745282560 | bytes 41435136 | tf_op jit(solution)/shard_map/dot_general | solution.py:21
  59.9 5.6 all-gather.15.cloned.1.call-done
  65.5 34.0 %multiply_convert_fusion.1 = (bf16[4096,2048]{1,0:T(8,128)(2,1)}, f32[4096,2048]{1,0:T(8,128)}) fusion(f32[4096,2048]{1,0:T(8,128)} %fusion.40, bf16[1,640,2048]{2,1,0:T(8,128)(2,1)} %all-gather.15.cloned.1.call-done, bf16[1,4096,640]{1,2,0:T(8,128)(2,1)} %copy.20, f32[4096]{0:T(1024)S(1)} %add_rsqrt_fusion), kind=kOutput, calls=%fused_computation.17 | convolution fusion | flops 10795614208 | bytes 91766784 | tf_op jit(solution)/shard_map/dot_general | solution.py:22
  99.5 18.6 %fusion.19 = (f32[4096]{0:T(1024)S(1)}, bf16[4096,640]{0,1:T(8,128)(2,1)}) fusion(bf16[4096,2048]{1,0:T(8,128)(2,1)} %get-tuple-element.30, bf16[1,2048,640]{2,1,0:T(8,128)(2,1)} %all-gather.17.cloned.1.call-done, bf16[1,4096,640]{1,2,0:T(8,128)(2,1)} %copy.20), kind=kOutput, calls=%fused_computation.37 | convolution fusion | flops 10750521344 | bytes 29900800 | tf_op jit(solution)/shard_map/dot_general | solution.py:10
  118.1 2.0 all-gather.21.cloned.1.call-done
  120.1 19.9 %convolution_convert_fusion.1 = bf16[4096,2048]{1,0:T(8,128)(2,1)} fusion(bf16[1,4096,640]{2,1,0:T(8,128)(2,1)} %param.12, bf16[1,2048,640]{2,1,0:T(8,128)(2,1)} %all-gather.21.cloned.1.call-done), kind=kOutput, calls=%fused_computation.29 | convolution fusion | flops 10745806848 | bytes 24641536 | tf_op jit(solution)/shard_map/transpose(jvp())/dot_general | solution.py:10
  140.0 7.4 %all-gather.23.cloned.1.call-done = bf16[1,640,2048]{2,1,0:T(8,128)(2,1)} async-done(((bf16[1,160,2048]{2,1,0:T(8,128)(2,1)}), bf16[1,640,2048]{2,1,0:T(8,128)(2,1)}) %all-gather.23.cloned.1.call-update) | async-done | bytes 2621456 | tf_op jit(solution)/shard_map/all_gather | solution.py:40
  147.3 21.8 %fusion.32 = f32[4096,2048]{1,0:T(8,128)} fusion(bf16[4096,640]{0,1:T(8,128)(2,1)} %get-tuple-element.33, f32[4096]{0:T(1024)S(1)} %fusion.89, bf16[1,640,2048]{2,1,0:T(8,128)(2,1)} %all-gather.23.cloned.1.call-done), kind=kOutput, calls=%fused_computation.52 | convolution fusion | flops 10745282560 | bytes 41435136 | tf_op jit(solution)/shard_map/jvp()/dot_general | solution.py:22
  169.1 5.5 all-gather.19.cloned.1.call-done
  174.6 44.7 %fusion.2 = (bf16[4096,2048]{1,0:T(8,128)(2,1)}, f32[4096,2048]{1,0:T(8,128)}) fusion(f32[4096,2048]{1,0:T(8,128)} %fusion.32, bf16[4096,2048]{1,0:T(8,128)(2,1)} %convolution_convert_fusion.1, bf16[1,640,2048]{2,1,0:T(8,128)(2,1)} %all-gather.19.cloned.1.call-done, bf16[4096,640]{0,1:T(8,128)(2,1)} %get-tuple-element.33, f32[4096]{0:T(1024)S(1)} %fusion.89), kind=kOutput, calls=%fused_computation.8 | convolution fusion | flops 10845945856 | bytes 108544000 | tf_op jit(solution)/shard_map/jvp()/dot_general | solution.py:21
  219.3 17.1 %convolution_convert_fusion.3 = bf16[4096,640]{0,1:T(8,128)(2,1)} fusion(bf16[4096,2048]{1,0:T(8,128)(2,1)} %get-tuple-element.34, bf16[1,640,2048]{2,1,0:T(8,128)(2,1)} %all-gather.19.cloned.1.call-done), kind=kOutput, calls=%fused_computation.42 | convolution fusion | flops 10737418240 | bytes 24641536 | tf_op jit(solution)/shard_map/transpose(jvp())/dot_general | solution.py:21
  236.4 25.6 %fusion.21 = (f32[4096]{0:T(1024)S(1)}, bf16[4096,640]{0,1:T(8,128)(2,1)}) fusion(bf16[4096,640]{0,1:T(8,128)(2,1)} %get-tuple-element.33, bf16[4096,640]{0,1:T(8,128)(2,1)} %convolution_convert_fusion.3, bf16[1,640,2048]{2,1,0:T(8,128)(2,1)S(1)} %copy-done.19, bf16[4096,2048]{1,0:T(8,128)(2,1)} %convolution_convert_fusion.1, ...), kind=kOutput, calls=%fused_computation.39 | convolution fusion | flops 10803474432 | bytes 68698112 | tf_op jit(solution)/shard_map/transpose(jvp())/dot_general | solution.py:22
  262.1 11.9 %fusion.26 = bf16[4096,640]{0,1:T(8,128)(2,1)} fusion(bf16[4096,640]{0,1:T(8,128)(2,1)} %get-tuple-element.33, bf16[4096,640]{0,1:T(8,128)(2,1)} %get-tuple-element.37, bf16[1,4096,640]{1,2,0:T(8,128)(2,1)} %copy.21, f32[4096]{0:T(1024)S(1)} %multiply_multiply_fusion.3, f32[4096]{0:T(1024)S(1)} %fusion.89), kind=kLoop, calls=%fused_computation.45 | loop fusion | flops 18350080 | bytes 21004288 | tf_op jit(solution)/shard_map/transpose(jvp())/add_any | solution.py:14
  274.0 19.6 %convolution_convert_fusion.4 = bf16[2048,640]{1,0:T(8,128)(2,1)} fusion(bf16[4096,2048]{1,0:T(8,128)(2,1)} %get-tuple-element.30, bf16[4096,640]{0,1:T(8,128)(2,1)} %fusion.26), kind=kOutput, calls=%fused_computation.71 | convolution fusion | flops 10738728960 | bytes 24641536 | tf_op jit(solution)/shard_map/transpose(jvp())/dot_general | solution.py:10
  293.6 0.0 reduce-scatter.15.cloned.1.call-update
  293.6 0.0 reduce-scatter.17.cloned.1.call-start
  293.6 27.2 %fusion.45 = bf16[2048,640]{1,0:T(8,128)(2,1)} fusion(bf16[1,4096,640]{2,1,0:T(8,128)(2,1)} %param.12, f32[4096,2048]{1,0:T(8,128)} %fusion.32, f32[4096,2048]{1,0:T(8,128)} %get-tuple-element.35), kind=kOutput, calls=%fused_computation.69 | convolution fusion | flops 10789060608 | bytes 74973184 | tf_op jit(solution)/shard_map/transpose(jvp())/dot_general | solution.py:10
  320.9 0.0 reduce-scatter.11.cloned.1.call-start
  320.9 18.8 %convolution_convert_fusion = bf16[4096,2048]{1,0:T(8,128)(2,1)} fusion(bf16[4096,640]{0,1:T(8,128)(2,1)} %fusion.26, bf16[1,2048,640]{2,1,0:T(8,128)(2,1)S(1)} %copy-done.18), kind=kOutput, calls=%fused_computation.28 | convolution fusion | flops 10745806848 | bytes 24641536 | tf_op jit(solution)/shard_map/transpose(jvp())/dot_general | solution.py:10
  339.7 22.4 %fusion.56 = bf16[640,2048]{1,0:T(8,128)(2,1)} fusion(bf16[4096,2048]{1,0:T(8,128)(2,1)} %convolution_convert_fusion, f32[4096,2048]{1,0:T(8,128)} %fusion.40, bf16[1,4096,640]{1,2,0:T(8,128)(2,1)} %copy.20, f32[4096]{0:T(1024)S(1)} %copy-done.17), kind=kOutput, calls=%fused_computation.73 | convolution fusion | flops 10796924928 | bytes 58212352 | tf_op jit(solution)/shard_map/transpose(jvp())/dot_general | solution.py:22
  362.1 0.0 reduce-scatter.13.cloned.1.call-start
  362.2 22.4 %fusion.48 = bf16[640,2048]{1,0:T(8,128)(2,1)} fusion(bf16[4096,2048]{1,0:T(8,128)(2,1)} %convolution_convert_fusion.1, bf16[4096,640]{0,1:T(8,128)(2,1)} %get-tuple-element.33, f32[4096]{0:T(1024)S(1)} %copy-done.13, f32[4096,2048]{1,0:T(8,128)} %get-tuple-element.35), kind=kOutput, calls=%fused_computation.70 | convolution fusion | flops 10796924928 | bytes 58212352 | tf_op jit(solution)/shard_map/transpose(jvp())/dot_general | solution.py:22
  384.6 0.0 reduce-scatter.7.cloned.1.call-start
  384.7 35.4 %fusion.51 = bf16[640,2048]{1,0:T(8,128)(2,1)} fusion(f32[4096,2048]{1,0:T(8,128)} %fusion.40, f32[4096,2048]{1,0:T(8,128)} %get-tuple-element.31, bf16[4096,2048]{1,0:T(8,128)(2,1)} %convolution_convert_fusion, bf16[1,4096,640]{1,2,0:T(8,128)(2,1)} %copy.20, f32[4096]{0:T(1024)S(1)} %copy-done.17), kind=kOutput, calls=%fused_computation.72 | convolution fusion | flops 10838867968 | bytes 91766784 | tf_op jit(solution)/shard_map/transpose(jvp())/dot_general | solution.py:21
  420.1 0.0 reduce-scatter.9.cloned.1.call-start
  420.1 17.1 %fusion.42 = bf16[640,2048]{1,0:T(8,128)(2,1)} fusion(bf16[4096,2048]{1,0:T(8,128)(2,1)} %get-tuple-element.34, bf16[4096,640]{0,1:T(8,128)(2,1)} %get-tuple-element.33, f32[4096]{0:T(1024)S(1)} %copy-done.13), kind=kOutput, calls=%fused_computation.68 | convolution fusion | flops 10745282560 | bytes 24657920 | tf_op jit(solution)/shard_map/transpose(jvp())/dot_general | solution.py:21
  437.2 0.0 all-reduce.3.cloned.1.call-start
  437.3 0.0 reduce-scatter.15.cloned.1.call-done
  437.3 0.0 reduce-scatter.17.cloned.1.call-done
  437.4 0.0 reduce-scatter.11.cloned.1.call-done
  437.4 2.6 reduce-scatter.13.cloned.1.call-done
  440.0 37.4 %reduce-scatter.7.cloned.1.call-done = bf16[160,2048]{1,0:T(8,128)(2,1)} async-done(((bf16[640,2048]{1,0:T(8,128)(2,1)}), bf16[160,2048]{1,0:T(8,128)(2,1)}) %reduce-scatter.7.cloned.1.call-update) | async-done | bytes 655376 | tf_op jit(solution)/shard_map/reduce_scatter | solution.py:43
  477.4 37.2 %reduce-scatter.9.cloned.1.call-done = bf16[160,2048]{1,0:T(8,128)(2,1)} async-done(((bf16[640,2048]{1,0:T(8,128)(2,1)}), bf16[160,2048]{1,0:T(8,128)(2,1)}) %reduce-scatter.9.cloned.1.call-update) | async-done | bytes 655376 | tf_op jit(solution)/shard_map/reduce_scatter | solution.py:43
  514.7 153.0 %all-reduce.3.cloned.1.call-done = (bf16[1,160,2048]{2,1,0:T(8,128)(2,1)}, bf16[1,160,2048]{2,1,0:T(8,128)(2,1)}, bf16[1,160,2048]{2,1,0:T(8,128)(2,1)}, bf16[1,...) async-done(((bf16[1,160,2048]{2,1,0:T(8,128)(2,1)}, bf16[1,160,2048]{2,1,0:T(8,128)(2,1)}, bf16[1,160,2048]{2,1,0:T(8,128)(2,1)}, ...) | async-done | bytes 3932176 | tf_op jit(solution)/shard_map/psum | solution.py:43
  667.7 2.6 fusion.70
  670.2 2.6 fusion.69
  672.8 2.7 fusion.68
  677.4 6.7 psum.55
  684.9 6.1 fusion.76
  691.0 1.3 copy-done.5
  692.4 0.7 copy-done.6
  693.1 0.7 copy-done.7
  693.9 0.1 copy-done.8
  693.9 0.2 copy-done.9
  694.1 6.3 fusion.67
  (46 shorter events, 0.2 us)
Async XLA Ops:
  7.2 5.3 copy-start
  7.2 30.9 %all-gather.13.cloned.1.call-start = ((), (), s32[]{:S(2)}) async-start(), calls=%async_computation.12 | async-start | bytes 3276800 | tf_op jit(solution)/shard_map/all_gather | solution.py:40
  9.8 55.7 %all-gather.15.cloned.1.call-start = ((), (), s32[]{:S(2)}) async-start(), calls=%async_computation.13 | async-start | bytes 3276800 | tf_op jit(solution)/shard_map/all_gather | solution.py:40
  12.4 87.1 %all-gather.17.cloned.1.call-start = ((), (), s32[]{:S(2)}) async-start(), calls=%async_computation.14 | async-start | bytes 3276800 | tf_op jit(solution)/shard_map/all_gather | solution.py:40
  13.7 106.5 %all-gather.21.cloned.1.call-start = ((), (), s32[]{:S(2)}) async-start(), calls=%async_computation.16 | async-start | bytes 3276800 | tf_op jit(solution)/shard_map/all_gather | solution.py:40
  14.2 133.1 %all-gather.23.cloned.1.call-start = ((), (), s32[]{:S(2)}) async-start(), calls=%async_computation.17 | async-start | bytes 3276800 | tf_op jit(solution)/shard_map/all_gather | solution.py:40
  14.8 159.7 %all-gather.19.cloned.1.call-start = ((), (), s32[]{:S(2)}) async-start(), calls=%async_computation.15 | async-start | bytes 3276800 | tf_op jit(solution)/shard_map/all_gather | solution.py:40
  15.4 421.9 %reduce-scatter.15.cloned.1.call-start = ((), (), s32[]{:S(2)}) async-start(), calls=%async_computation.10 | async-start | bytes 3276800 | tf_op jit(solution)/shard_map/reduce_scatter | solution.py:43
  27.0 38.5 %copy-start.16 = (f32[4096]{0:T(1024)}, f32[4096]{0:T(1024)S(1)}, u32[]{:S(2)}) copy-start(f32[4096]{0:T(1024)S(1)} %add_rsqrt_fusion) | copy-start | bytes 49156
  118.1 21.9 %copy-start.14 = (f32[4096]{0:T(1024)}, f32[4096]{0:T(1024)S(1)}, u32[]{:S(2)}) copy-start(f32[4096]{0:T(1024)S(1)} %get-tuple-element.32) | copy-start | bytes 49156
  118.1 143.9 %copy-start.12 = (f32[4096]{0:T(1024)}, f32[4096]{0:T(1024)S(1)}, u32[]{:S(2)}) copy-start(f32[4096]{0:T(1024)S(1)} %fusion.89) | copy-start | bytes 49156
  219.3 17.1 %copy-start.19 = (bf16[1,640,2048]{2,1,0:T(8,128)(2,1)S(1)}, bf16[1,640,2048]{2,1,0:T(8,128)(2,1)}, u32[]{:S(2)}) copy-start(bf16[1,640,2048]{2,1,0:T(8,128)(2,1)} %all-gather.23.cloned.1.call-done) | copy-start | bytes 7864324
  236.4 25.6 %copy-start.15 = (f32[4096]{0:T(1024)S(1)}, f32[4096]{0:T(1024)}, u32[]{:S(2)}) copy-start(f32[4096]{0:T(1024)} %copy-done.14) | copy-start | bytes 49156
  293.6 27.3 %copy-start.18 = (bf16[1,2048,640]{2,1,0:T(8,128)(2,1)S(1)}, bf16[1,2048,640]{2,1,0:T(8,128)(2,1)}, u32[]{:S(2)}) copy-start(bf16[1,2048,640]{2,1,0:T(8,128)(2,1)} %all-gather.17.cloned.1.call-done) | copy-start | bytes 7864324
  293.6 143.8 %reduce-scatter.17.cloned.1.call-start = ((), (), s32[]{:S(2)}) async-start(), calls=%async_computation.11 | async-start | bytes 3276800 | tf_op jit(solution)/shard_map/reduce_scatter | solution.py:43
  320.9 18.9 %copy-start.17 = (f32[4096]{0:T(1024)S(1)}, f32[4096]{0:T(1024)}, u32[]{:S(2)}) copy-start(f32[4096]{0:T(1024)} %copy-done.16) | copy-start | bytes 49156
  320.9 116.5 %reduce-scatter.11.cloned.1.call-start = ((), (), s32[]{:S(2)}) async-start(), calls=%async_computation.8 | async-start | bytes 3276800 | tf_op jit(solution)/shard_map/reduce_scatter | solution.py:43
  339.7 22.5 %copy-start.13 = (f32[4096]{0:T(1024)S(1)}, f32[4096]{0:T(1024)}, u32[]{:S(2)}) copy-start(f32[4096]{0:T(1024)} %copy-done.12) | copy-start | bytes 49156
  362.1 77.8 %reduce-scatter.13.cloned.1.call-start = ((), (), s32[]{:S(2)}) async-start(), calls=%async_computation.9 | async-start | bytes 3276800 | tf_op jit(solution)/shard_map/reduce_scatter | solution.py:43
  384.6 92.8 %reduce-scatter.7.cloned.1.call-start = ((), (), s32[]{:S(2)}) async-start(), calls=%async_computation.6 | async-start | bytes 3276800 | tf_op jit(solution)/shard_map/reduce_scatter | solution.py:43
  420.1 94.6 %reduce-scatter.9.cloned.1.call-start = ((), (), s32[]{:S(2)}) async-start(), calls=%async_computation.7 | async-start | bytes 3276800 | tf_op jit(solution)/shard_map/reduce_scatter | solution.py:43
  437.2 247.6 %copy-start.1 = (bf16[2,512,640]{2,1,0:T(8,128)(2,1)S(1)}, bf16[2,512,640]{2,1,0:T(8,128)(2,1)}, u32[]{:S(2)}) copy-start(bf16[2,512,640]{2,1,0:T(8,128)(2,1)} %param.15) | copy-start | bytes 3932164
  437.2 230.4 %all-reduce.3.cloned.1.call-start = ((), (), s32[]{:S(2)}) async-start(), calls=%async_computation.18 | async-start | bytes 7864320 | tf_op jit(solution)/shard_map/psum | solution.py:43
  672.8 18.2 %copy-start.10 = (bf16[1,160,2048]{2,1,0:T(8,128)(2,1)S(1)}, bf16[1,160,2048]{2,1,0:T(8,128)(2,1)}, u32[]{:S(2)}) copy-start(bf16[1,160,2048]{2,1,0:T(8,128)(2,1)} %get-tuple-element.11) | copy-start | bytes 1966084
  672.8 18.2 %copy-start.11 = (bf16[1,160,2048]{2,1,0:T(8,128)(2,1)S(1)}, bf16[1,160,2048]{2,1,0:T(8,128)(2,1)}, u32[]{:S(2)}) copy-start(bf16[1,160,2048]{2,1,0:T(8,128)(2,1)} %get-tuple-element.12) | copy-start | bytes 1966084
  684.8 6.2 copy-start.2
  684.8 6.2 copy-start.3
  684.8 6.2 copy-start.4
  684.8 7.6 %copy-start.5 = (f32[2,160,2048]{2,1,0:T(8,128)S(1)}, f32[2,160,2048]{2,1,0:T(8,128)}, u32[]{:S(2)}) copy-start(f32[2,160,2048]{2,1,0:T(8,128)} %param.16) | copy-start | bytes 7864324
  684.8 8.3 %copy-start.6 = (f32[2,160,2048]{2,1,0:T(8,128)S(1)}, f32[2,160,2048]{2,1,0:T(8,128)}, u32[]{:S(2)}) copy-start(f32[2,160,2048]{2,1,0:T(8,128)} %param.20) | copy-start | bytes 7864324
  684.8 9.0 %copy-start.7 = (f32[2,160,2048]{2,1,0:T(8,128)S(1)}, f32[2,160,2048]{2,1,0:T(8,128)}, u32[]{:S(2)}) copy-start(f32[2,160,2048]{2,1,0:T(8,128)} %param.17) | copy-start | bytes 7864324
  684.9 9.1 %copy-start.8 = (bf16[1,160,2048]{2,1,0:T(8,128)(2,1)S(1)}, bf16[1,160,2048]{2,1,0:T(8,128)(2,1)}, u32[]{:S(2)}) copy-start(bf16[1,160,2048]{2,1,0:T(8,128)(2,1)} %get-tuple-element.9) | copy-start | bytes 1966084
  684.9 9.3 %copy-start.9 = (bf16[1,160,2048]{2,1,0:T(8,128)(2,1)S(1)}, bf16[1,160,2048]{2,1,0:T(8,128)(2,1)}, u32[]{:S(2)}) copy-start(bf16[1,160,2048]{2,1,0:T(8,128)(2,1)} %get-tuple-element.10) | copy-start | bytes 1966084
Sparse Core Ops, SparseCore 0:
  10.1 27.9 all-gather.12
  40.3 25.1 all-gather.14
  67.6 25.1 all-gather.16
  94.9 25.1 all-gather.20
  122.1 25.1 all-gather.22
  149.3 25.1 all-gather.18
  293.7 34.2 reduce-scatter.14
  331.1 34.2 reduce-scatter.16
  368.5 34.2 reduce-scatter.10
  405.7 34.2 reduce-scatter.12
  443.1 34.2 reduce-scatter.6
  480.4 34.2 reduce-scatter.8
  518.9 148.6 all-reduce.2
where the time goes:
time: 715 us; the launch traced here: 707 us
  matrix products  366 us (51%)
  waiting for transfers between devices  256 us (36%)
  other arithmetic  35.7 us (5%)
  local copies, waits for them, and re-layouts  25.4 us (4%)
  between operations  17.3 us (2%)
    psum x1, waiting for transfers between devices, summed(): lax.psum(lax.psum_scatter(term, 's', scatter_dimension=0, tiled=True), 'r')  153 us
    dot_general x5, matrix products, layer(): gate = jnp.dot(a, w['w_gate'], preferred_element_type=jnp.float32)  136 us
    dot_general x5, matrix products, layer(): up = jnp.dot(a, w['w_up'], preferred_element_type=jnp.float32)  126 us
    dot_general x5, matrix products, matmul(): jnp.dot(a, w, preferred_element_type=jnp.float32).astype(jnp.bfloat16)  104 us
    reduce_scatter x6, waiting for transfers between devices, summed(): lax.psum_scatter(term, 's', scatter_dimension=0, tiled=True)  77.3 us
    all_gather x6, waiting for transfers between devices, fetched(): lax.all_gather(w[number], 's', axis=0, tiled=True)  23.5 us
    unnamed x42, local copies, waits for them, and re-layouts  19.1 us
  transfers between devices with their start and end apart: 13, of which 9 were waited for; matrix products, arithmetic and copies ran while one was open for 40% of the time, Pallas kernels for 0%

commit v1 on v0

v1 whole, which is shorter than its diff:
```python
import functools

import jax
import jax.numpy as jnp
from jax import lax
from jax.experimental import pallas as pl
from jax.experimental.pallas import tpu as pltpu
from jax.sharding import PartitionSpec as P

F32, BF16 = jnp.float32, jnp.bfloat16
MESH = pl.DeviceIdType.MESH
LIMIT = 66_000_000
NT = (((1,), (1,)), ((), ()))
TOKENS_F, TOKENS_B = 512, 1024
LANES, WIDE, HALF, OWN = 128, 512, 240, 160
THREE = range(3)
STEPS_Z = (1, 2, 3)


def dot(a, b):
    return jnp.dot(a, b, preferred_element_type=F32)


def dot_nt(a, b):
    return lax.dot_general(a, b, NT, preferred_element_type=F32)


def sigmoid(g):
    return 0.5 * jnp.tanh(0.5 * g) + 0.5


def scale_of(wide):
    return lax.rsqrt(jnp.mean(wide * wide, -1, keepdims=True) + 1e-6)


def keep(ref, value, q):
    for c in range(4):
        ref[0, c, :, LANES * q : LANES * q + LANES] = value[:, LANES * c : LANES * c + LANES]


def forward_kernel(x_ref, g_block, u_block, d_block, h_ref, at_ref, g_ref, u_ref, wg_all, wu_all, wd_all, z_ref, *scratch):
    own, held, sems_s, sems_r, sems_own, sems_held = scratch[:3], scratch[3:6], *scratch[6:]
    step, steps = pl.program_id(0), pl.num_programs(0)
    rep, r, s = lax.axis_index("rep"), lax.axis_index("r"), lax.axis_index("s")
    ax, core, ay, az = s // 2, s % 2, r // 4, r % 4
    mate = (rep, r, ax * 2 + 1 - core)
    far = (1 - ax) * 2 + core
    across = (rep, r, far)
    over = (rep, (1 - ay) * 4 + az, s)
    blocks, alls, halves = (g_block, u_block, d_block), (wg_all, wu_all, wd_all), (80, 80, 256)

    def half(i, layer, place, which):
        n = halves[i]
        return alls[i].at[layer, pl.ds(pl.multiple_of(2 * n * place + n * which, 16), n)]

    def copy(kind, i, layer, src, dst, who):
        return pltpu.make_async_remote_copy(
            src_ref=src,
            dst_ref=dst,
            send_sem=sems_s.at[kind, layer, i],
            recv_sem=sems_r.at[kind, layer, i],
            device_id=who,
            device_id_type=MESH,
        )

    def whole_block(i, layer, place):
        n = 2 * halves[i]
        return alls[i].at[layer, pl.ds(pl.multiple_of(n * place, 16), n)]

    def to_mate(i, layer):
        return copy(0, i, layer, blocks[i].at[layer], whole_block(i, layer, s), mate)

    def to_across(i, layer):
        n = halves[i]
        return copy(1, i, layer, blocks[i].at[layer, pl.ds(pl.multiple_of(n * ay, 16), n)], half(i, layer, s, ay), across)

    def to_over(i, layer):
        return copy(2, i, layer, half(i, layer, far, ay), half(i, layer, far, ay), over)

    def near_on(i, layer):
        return copy(3, i, layer, half(i, layer, far, ay), half(i, layer, far, ay), mate)

    def far_on(i, layer):
        return copy(4, i, layer, half(i, layer, far, 1 - ay), half(i, layer, far, 1 - ay), mate)

    def own_in(i, layer):
        return pltpu.make_async_copy(blocks[i].at[layer], own[i].at[layer], sems_own.at[0, layer, i])

    def own_out(i, layer):
        return pltpu.make_async_copy(own[i].at[layer], whole_block(i, layer, s), sems_own.at[1, layer, i])

    def first_half(layer):
        for i in THREE:
            to_across(i, layer).wait_recv()
            to_over(i, layer).start()
            near_on(i, layer).start()

    def second_half(layer):
        for i in THREE:
            to_over(i, layer).wait_recv()
            far_on(i, layer).start()

    def finish(layer):
        for i in THREE:
            to_across(i, layer).wait_send()
            to_over(i, layer).wait_send()
            to_mate(i, layer).wait()
            near_on(i, layer).wait()
            far_on(i, layer).wait()
            own_out(i, layer).wait()

    @pl.when(step == 0)
    def _():
        for layer in range(2):
            for i in THREE:
                own_in(i, layer).start()
        barrier = pltpu.get_barrier_semaphore()
        for who in (mate, across, over):
            pl.semaphore_signal(barrier, inc=1, device_id=who, device_id_type=MESH)
        pl.semaphore_wait(barrier, 3)
        for layer in range(2):
            for i in THREE:
                to_across(i, layer).start()
        for layer in range(2):
            for i in THREE:
                to_mate(i, layer).start()
                own_in(i, layer).wait()
                own_out(i, layer).start()
        first_half(0)
        second_half(0)
        finish(0)
        loads = [pltpu.make_async_copy(alls[i].at[0], held[i], sems_held.at[i]) for i in THREE]
        for load in loads:
            load.start()
        for load in loads:
            load.wait()

    @pl.when(step == 1)
    def _():
        first_half(1)

    @pl.when(step == 3)
    def _():
        second_half(1)

    @pl.when(step == steps - 1)
    def _():
        finish(1)

    wg_ref, wu_ref, wd_ref = held
    x = x_ref[...]
    wide = x.astype(F32)
    a = (wide * scale_of(wide)).astype(BF16)
    at_ref[0] = a.T
    for q in range(4):
        cols = slice(WIDE * q, WIDE * q + WIDE)
        gate = dot(a, wg_ref[:, cols])
        up = dot(a, wu_ref[:, cols])
        keep(g_ref, gate, q)
        keep(u_ref, up, q)
        z_ref[:, cols] = (gate * sigmoid(gate) * up).astype(BF16)
    out = dot(z_ref[...], wd_ref[...]).astype(BF16)
    h_ref[...] = (wide + out.astype(F32)).astype(BF16)


def grads(gate, up, dz):
    s = sigmoid(gate)
    silu = gate * s
    dup = dz * silu
    dgate = dz * up * (s + silu * (1.0 - s))
    return silu * up, dgate, dup


def turn_kernel(h_ref, dy_ref, wg_ref, wu_ref, wd_ref, at_in, g_in, u_in, dys_ref, dyt_ref, at_ref, g_ref, u_ref, dg_ref, du_ref):
    wide = h_ref[...].astype(F32)
    scale = scale_of(wide)
    a = (wide * scale).astype(BF16)
    at_ref[0] = a.T
    dy = dy_ref[...]
    for q in range(4):
        cols = slice(WIDE * q, WIDE * q + WIDE)
        gate = dot(a, wg_ref[:, cols])
        up = dot(a, wu_ref[:, cols])
        dz = dot_nt(dy, wd_ref[cols, :]).astype(BF16).astype(F32)
        keep(g_ref, gate, q)
        keep(u_ref, up, q)
        _, dgate, dup = grads(gate, up, dz)
        dg_ref[:, cols] = dgate.astype(BF16)
        du_ref[:, cols] = dup.astype(BF16)
    da = dot_nt(dg_ref[...], wg_ref[...]) + dot_nt(du_ref[...], wu_ref[...])
    dot_mean = jnp.mean(da * wide, -1, keepdims=True)
    dh = da * scale - wide * (scale * scale * scale * dot_mean)
    dh = (dy.astype(F32) + dh).astype(BF16)
    dys_ref[1] = dy
    dys_ref[0] = dh
    dyt_ref[1] = dy.T
    dyt_ref[0] = dh.T


def forward(x, wg, wu, wd):
    n, d = x.shape
    f = wg.shape[2]
    t = TOKENS_F
    row = pl.BlockSpec((t, d), lambda i: (i, 0))
    kept = pl.BlockSpec((1, 4, t, f // 4), lambda i: (0, 0, i, 0))
    hbm = pl.BlockSpec(memory_space=pl.ANY)
    return pl.pallas_call(
        forward_kernel,
        grid=(n // t,),
        in_specs=[row, hbm, hbm, hbm],
        out_specs=[row, pl.BlockSpec((1, d, t), lambda i: (0, 0, i)), kept, kept, hbm, hbm, hbm],
        out_shape=[
            jax.ShapeDtypeStruct((n, d), BF16),
            jax.ShapeDtypeStruct((2, d, n), BF16),
            jax.ShapeDtypeStruct((2, 4, n, f // 4), F32),
            jax.ShapeDtypeStruct((2, 4, n, f // 4), F32),
            jax.ShapeDtypeStruct((2, d, f), BF16),
            jax.ShapeDtypeStruct((2, d, f), BF16),
            jax.ShapeDtypeStruct((2, f, d), BF16),
        ],
        scratch_shapes=[
            pltpu.VMEM((t, f), BF16),
            *[pltpu.VMEM(w.shape, BF16) for w in (wg, wu, wd)],
            pltpu.VMEM((d, f), BF16),
            pltpu.VMEM((d, f), BF16),
            pltpu.VMEM((f, d), BF16),
            pltpu.SemaphoreType.DMA((5, 2, 3)),
            pltpu.SemaphoreType.DMA((5, 2, 3)),
            pltpu.SemaphoreType.DMA((2, 2, 3)),
            pltpu.SemaphoreType.DMA((3,)),
        ],
        compiler_params=pltpu.CompilerParams(vmem_limit_bytes=LIMIT, collective_id=0, has_side_effects=True),
        cost_estimate=pl.CostEstimate(flops=6 * n * d * f, bytes_accessed=100_000_000, transcendentals=0),
        name="forward",
    )(x, wg, wu, wd)


def turn(h, dy, wg, wu, wd, at, g, u):
    n, d = h.shape
    f = wg.shape[2]
    t = TOKENS_F
    whole = lambda s: pl.BlockSpec((None, *s), lambda i: (1, 0, 0), pipeline_mode=pl.Buffered(1))
    row = pl.BlockSpec((t, d), lambda i: (i, 0))
    kept = pl.BlockSpec((1, 4, t, f // 4), lambda i: (1, 0, i, 0))
    hbm = pl.BlockSpec(memory_space=pl.ANY)
    return pl.pallas_call(
        turn_kernel,
        grid=(n // t,),
        in_specs=[row, row, whole((d, f)), whole((d, f)), whole((f, d)), hbm, hbm, hbm],
        out_specs=[
            pl.BlockSpec((2, t, d), lambda i: (0, i, 0)),
            pl.BlockSpec((2, d, t), lambda i: (0, 0, i)),
            pl.BlockSpec((1, d, t), lambda i: (1, 0, i)),
            kept,
            kept,
        ],
        out_shape=[
            jax.ShapeDtypeStruct((2, n, d), BF16),
            jax.ShapeDtypeStruct((2, d, n), BF16),
            jax.ShapeDtypeStruct((2, d, n), BF16),
            jax.ShapeDtypeStruct((2, 4, n, f // 4), F32),
            jax.ShapeDtypeStruct((2, 4, n, f // 4), F32),
        ],
        input_output_aliases={5: 2, 6: 3, 7: 4},
        scratch_shapes=[pltpu.VMEM((t, f), BF16)] * 2,
        compiler_params=pltpu.CompilerParams(vmem_limit_bytes=LIMIT),
        cost_estimate=pl.CostEstimate(flops=10 * n * d * f, bytes_accessed=100_000_000, transcendentals=0),
        name="turn",
    )(h, dy, wg, wu, wd, at, g, u)


TICKS = 4
PIECES = 4
t_b = TOKENS_B // PIECES
CHUNKS = 8


def sum_kernel(dys_ref, dyt_ref, at_ref, g_ref, u_ref, wd_ref, out_ref, sq_ref, acc, p, rc, q, rx, sy, ry, sz, rz, sems_s, sems_r, zs, dgs, dus, sqz, sqp, sqr, sq_s, sq_r, fin, fin_s):
    tick = pl.program_id(0)
    chunk, part = tick // TICKS, tick % TICKS
    rep, r, s = lax.axis_index("rep"), lax.axis_index("r"), lax.axis_index("s")
    x, core, y, z = s // 2, s % 2, r // 4, r % 4
    mate = (rep, r, x * 2 + 1 - core)
    across = (rep, r, (1 - x) * 2 + core)
    over = (rep, (1 - y) * 4 + z, s)
    others = [(rep, y * 4 + (z + k) % 4, s) for k in STEPS_Z]

    @pl.when(tick == 0)
    def _():
        barrier = pltpu.get_barrier_semaphore()
        for who in [mate, across, over, *others]:
            pl.semaphore_signal(barrier, inc=1, device_id=who, device_id_type=MESH)
        pl.semaphore_wait(barrier, 6)
        sq_ref[...] = jnp.zeros_like(sq_ref)

    def copy(src, dst, kind, j, who):
        return pltpu.make_async_remote_copy(
            src_ref=src, dst_ref=dst, send_sem=sems_s.at[kind, j], recv_sem=sems_r.at[kind, j], device_id=who, device_id_type=MESH
        )

    def by_core(j):
        return copy(p.at[j % 2, 1 - core], rc.at[j], 0, j, mate)

    def by_x(j):
        return copy(q.at[j % 2, 1 - x], rx.at[j], 1, j, across)

    def by_y(j):
        return copy(sy.at[j % 2, 1 - y], ry.at[j], 2, j, over)

    def by_z(j, k):
        return copy(sz.at[j % 2, (z + k) % 4], rz.at[j, k - 1], 2 + k, j, others[k - 1])

    def all_z(j, k):
        return copy(fin.at[j, y, z], fin.at[j, y, z], 5 + k, j, others[k - 1])

    def all_y(j):
        return copy(fin.at[j, y], fin.at[j, y], 9, j, over)

    def square(src, dst, kind, who):
        return pltpu.make_async_remote_copy(
            src_ref=src, dst_ref=dst, send_sem=sq_s.at[kind], recv_sem=sq_r.at[kind], device_id=who, device_id_type=MESH
        )

    def squares_z(k):
        return square(sqz.at[z], sqz.at[z], k - 1, others[k - 1])

    def squares(k):
        return square(sqp.at[k], sqr.at[k], 3 + k, (over, across, mate)[k])

    def give(j):
        return pltpu.make_async_copy(fin.at[j], out_ref.at[j], fin_s.at[j])

    def at(rounds, when, j_ok=True):
        j = chunk - rounds
        return j, (part == when) & (j >= 0) & (j < CHUNKS)

    j, now = at(1, 0)

    @pl.when(now)
    def _():
        by_core(j).wait()
        for k in range(2):
            q[j % 2, k] = (p[j % 2, core, k].astype(F32) + rc[j, k].astype(F32)).astype(BF16)
        by_x(j).start()

    j, now = at(2, 0)

    @pl.when(now)
    def _():
        by_x(j).wait()
        total = (q[j % 2, x].astype(F32) + rx[j].astype(F32)).astype(BF16)
        for k in range(2):
            for i in range(4):
                sy[j % 2, k, i] = total[HALF * k : HALF * k + HALF, LANES * i : LANES * i + LANES]
        by_y(j).start()

    j, now = at(2, 2)

    @pl.when(now)
    def _():
        by_y(j).wait()
        sz[j % 2] = (sy[j % 2, y].astype(F32) + ry[j].astype(F32)).astype(BF16)
        for k in STEPS_Z:
            by_z(j, k).start()

    j, now = at(3, 0)

    @pl.when(now)
    def _():
        for k in STEPS_Z:
            by_z(j, k).wait()
        total = sz[j % 2, z].astype(F32)
        for k in THREE:
            total += rz[j, k].astype(F32)
        total = total.astype(BF16)
        fin[j, y, z] = total
        total = total.astype(F32)
        sq_ref[...] += jnp.sum((total * total).reshape(30, 8, LANES), 0)
        for k in STEPS_Z:
            all_z(j, k).start()

        @pl.when(j == CHUNKS - 1)
        def _():
            sqz[z] = sq_ref[...]
            for k in STEPS_Z:
                squares_z(k).start()

    j, now = at(3, 2)

    @pl.when(now)
    def _():
        for k in STEPS_Z:
            all_z(j, k).wait()
        all_y(j).start()

        @pl.when(j == CHUNKS - 1)
        def _():
            for k in STEPS_Z:
                squares_z(k).wait()
            total = (sqz[0] + sqz[1]) + (sqz[2] + sqz[3])
            for k in THREE:
                sqp[k] = total
                squares(k).start()
                squares(k).wait()
                total = total + sqr[k]
            sq_ref[...] = total

    j, now = at(4, 0)

    @pl.when(now)
    def _():
        all_y(j).wait()
        give(j).start()

    @pl.when(tick == pl.num_programs(0) - 1)
    def _():
        for j in range(CHUNKS):
            give(j).wait()

    @pl.when(chunk < CHUNKS)
    def _():
        @pl.when(part == 0)
        def _():
            acc[...] = jnp.zeros_like(acc)

        w = wd_ref[0, :, 0].reshape(WIDE, 640)
        for i in range(PIECES):
            rows = slice(t_b * i, t_b * i + t_b)
            dz = dot_nt(dys_ref[0, rows], w).astype(BF16).astype(F32)
            for ref, value in zip((zs, dgs, dus), grads(g_ref[0, 0, rows], u_ref[0, 0, rows], dz), strict=True):
                ref[rows] = value.astype(BF16)
        acc[0] += dot(at_ref[0], dgs[...])
        acc[1] += dot(at_ref[0], dus[...])
        acc[2] += dot(dyt_ref[0], zs[...])

        @pl.when(part == TICKS - 1)
        def _():
            for b in range(4):
                rows = slice(OWN * b, OWN * b + OWN)
                cols = slice(LANES * b, LANES * b + LANES)
                for k in range(2):
                    p[chunk % 2, b % 2, b // 2, OWN * k : OWN * k + OWN] = acc[k, rows].astype(BF16)
                for i in range(4):
                    down = slice(OWN * i, OWN * i + OWN)
                    p[chunk % 2, b % 2, b // 2, 320:480, LANES * i : LANES * i + LANES] = acc[2, down, cols].astype(BF16)
            by_core(chunk).start()


def summed(dys, dyt, at, g, u, wd):
    n, d = dys.shape[1:]
    t = TOKENS_B
    last = CHUNKS * TICKS - 1
    steps = CHUNKS * TICKS + 3 * TICKS + 1

    def where(i):
        i = jnp.minimum(i, last)
        return 1 - i // (4 * TICKS), (i // TICKS) % 4, i % TICKS

    def spec(shape, pick):
        return pl.BlockSpec(shape, lambda i: pick(*where(i)))

    kept = spec((1, 1, t, WIDE), lambda l, c, k: (l, c, k, 0))
    wide = spec((1, d, t), lambda l, c, k: (l, 0, k))
    vmem = pl.BlockSpec(memory_space=pltpu.VMEM)
    return pl.pallas_call(
        sum_kernel,
        grid=(steps,),
        in_specs=[
            spec((1, t, d), lambda l, c, k: (l, k, 0)),
            wide,
            wide,
            kept,
            kept,
            spec((1, 4, 1, LANES, d), lambda l, c, k: (l, 0, c, 0, 0)),
        ],
        out_specs=[pl.BlockSpec(memory_space=pl.ANY), vmem],
        out_shape=[jax.ShapeDtypeStruct((CHUNKS, 2, 4, HALF, LANES), BF16), jax.ShapeDtypeStruct((8, LANES), F32)],
        scratch_shapes=[
            pltpu.VMEM((3, d, WIDE), F32),
            pltpu.VMEM((2, 2, 2, 480, WIDE), BF16),
            pltpu.VMEM((CHUNKS, 2, 480, WIDE), BF16),
            pltpu.VMEM((2, 2, 480, WIDE), BF16),
            pltpu.VMEM((CHUNKS, 480, WIDE), BF16),
            pltpu.VMEM((2, 2, 4, HALF, LANES), BF16),
            pltpu.VMEM((CHUNKS, 4, HALF, LANES), BF16),
            pltpu.VMEM((2, 4, HALF, LANES), BF16),
            pltpu.VMEM((CHUNKS, 3, HALF, LANES), BF16),
            pltpu.SemaphoreType.DMA((10, CHUNKS)),
            pltpu.SemaphoreType.DMA((10, CHUNKS)),
            *[pltpu.VMEM((TOKENS_B, WIDE), BF16)] * 3,
            pltpu.VMEM((4, 8, LANES), F32),
            pltpu.VMEM((3, 8, LANES), F32),
            pltpu.VMEM((3, 8, LANES), F32),
            pltpu.SemaphoreType.DMA((6,)),
            pltpu.SemaphoreType.DMA((6,)),
            pltpu.VMEM((CHUNKS, 2, 4, HALF, LANES), BF16),
            pltpu.SemaphoreType.DMA((CHUNKS,)),
        ],
        compiler_params=pltpu.CompilerParams(vmem_limit_bytes=LIMIT, collective_id=1, has_side_effects=True),
        cost_estimate=pl.CostEstimate(flops=16 * n * d * 2048, bytes_accessed=200_000_000, transcendentals=0),
        name="summed",
    )(dys, dyt, at, g, u, wd)


def adamw(w, m, v, g):
    m = 0.9 * m + 0.1 * g
    v = 0.95 * v + 0.05 * g * g
    step = m * lax.rsqrt(v + 1e-8) + 0.1 * w
    return (w - 0.02 * step).astype(BF16), m, v


def step_kernel(count, squares_ref, grad_ref, *refs):
    w, m, v, new_w, new_m, new_v = (refs[3 * i : 3 * i + 3] for i in range(6))
    squares = jnp.sum(jnp.sum(squares_ref[...], 0, keepdims=True), 1, keepdims=True)
    factor = jnp.minimum(1.0, 0.5 * lax.rsqrt(squares / count + 1e-30))
    half = pl.program_id(1)

    def apply(i, at, g):
        out = adamw(w[i][at].astype(F32), m[i][at], v[i][at], g.astype(F32) * factor)
        for ref, value in zip((new_w[i], new_m[i], new_v[i]), out, strict=True):
            ref[at] = value

    for c in range(4):
        for z in range(4):
            cols = slice(WIDE * z + LANES * c, WIDE * z + LANES * c + LANES)
            apply(0, (0, slice(None), cols), grad_ref[c, 0, z, pl.ds(pl.multiple_of(80 * half, 16), 80)])
            up_at = pl.ds(pl.multiple_of(OWN * (1 - half), 16), 80)
            apply(1, (0, slice(None), cols), grad_ref[c, half, z, up_at])
    for k in range(2):
        c = 2 * half + k
        turned = jnp.concatenate([grad_ref[c, 1, z, 80:HALF].astype(F32) for z in range(4)], 0).T
        apply(2, (0, slice(LANES * k, LANES * k + LANES)), turned)


def stepped(squares, grad, weights, m, v):
    layers, rows, f = weights[0].shape
    down = weights[2].shape[1:]
    a = pl.BlockSpec((1, rows // 2, f), lambda l, k: (l, k, 0))
    b = pl.BlockSpec((1, down[0] // 2, down[1]), lambda l, k: (l, k, 0))
    three = [a, a, b]
    shapes = [jax.ShapeDtypeStruct(w.shape, t) for t in (BF16, F32, F32) for w in weights]
    return pl.pallas_call(
        functools.partial(step_kernel, 4.0 * sum(w.size for w in weights)),
        grid=(layers, 2),
        in_specs=[
            pl.BlockSpec((8, LANES), lambda l, k: (0, 0)),
            pl.BlockSpec((4, 2, 4, HALF, LANES), lambda l, k: (1 - l, 0, 0, 0, 0)),
            *(three * 3),
        ],
        out_specs=three * 3,
        out_shape=shapes,
        compiler_params=pltpu.CompilerParams(vmem_limit_bytes=LIMIT),
        cost_estimate=pl.CostEstimate(flops=30_000_000, bytes_accessed=43_000_000, transcendentals=0),
        name="stepped",
    )(squares, grad, *weights, *m, *v)


def solution(mesh):
    def step(x, dy, *arrays):
        weights, m, v = (arrays[i : i + 3] for i in (0, 3, 6))
        h, at, g, u, wg, wu, wd = forward(x[0], *weights)
        dys, dyt, at, g, u = turn(h, dy[0], wg, wu, wd, at, g, u)
        grad, squares = summed(dys, dyt, at, g, u, wd.reshape(2, 4, 4, LANES, 640))
        return tuple(stepped(squares, grad, weights, m, v))

    states, cut = P(("rep", "r", "s"), None, None), P(None, "s", None)
    return jax.shard_map(
        step,
        mesh=mesh,
        in_specs=(states, states) + (cut,) * 9,
        out_specs=(P("rep", "s", None),) * 9,
        check_vma=False,
    )
```

time: 715 us -> 395 us (0.55); the launches traced: 707 us -> 395 us
  Pallas kernels: 0 us -> 394 us
  matrix products: 366 us -> 0 us
  waiting for transfers between devices: 256 us -> 0 us
  other arithmetic: 35.7 us -> 0 us
  local copies, waits for them, and re-layouts: 25.4 us -> 0 us
  between operations: 17.3 us -> 0.84 us
    pallas_call x0 -> x4, Pallas kernels: none -> 394 us  [the longest x1 191 us: summed(): pl.pallas_call(sum_kernel, grid=(steps,), in_specs=[spec((1, t, d), lambd...]
    dot_general x15 -> x0, matrix products: 366 us -> none  [the longest x5 136 us: layer(): gate = jnp.dot(a, w['w_gate'], preferred_element_type=jnp.float32)]
    psum x1 -> x0, waiting for transfers between devices: 153 us -> none  [summed(): lax.psum(lax.psum_scatter(term, 's', scatter_dimension=0, tiled=True), 'r')]
    reduce_scatter x6 -> x0, waiting for transfers between devices: 77.3 us -> none  [summed(): lax.psum_scatter(term, 's', scatter_dimension=0, tiled=True)]
    all_gather x6 -> x0, waiting for transfers between devices: 23.5 us -> none  [fetched(): lax.all_gather(w[number], 's', axis=0, tiled=True)]
    unnamed x42 -> x0, local copies, waits for them, and re-layouts: 19.1 us -> none
    convert_element_type x2 -> x0, other arithmetic: 12.4 us -> none  [adamw(): return ((w - 0.02 * step).astype(jnp.bfloat16), m, v)]
    add_any x1 -> x0, other arithmetic: 11.9 us -> none  [normed(): wide = h.astype(jnp.float32)]
  transfers between devices with their start and end apart: 13 -> 0, of which waited for: 9 -> 0; matrix products, arithmetic and copies ran while one was open for 40% -> 0% of each run, Pallas kernels for 0% -> 0%
where the time goes in v1:
time: 395 us
  Pallas kernels  394 us (100%)
    pallas_call x1, Pallas kernels, summed(): pl.pallas_call(sum_kernel, grid=(steps,), in_specs=[spec((1, t, d), lambd...  191 us
    pallas_call x1, Pallas kernels, forward(): pl.pallas_call(forward_kernel, grid=(n // t,), in_specs=[row, hbm, hbm, h...  99.6 us
    pallas_call x1, Pallas kernels, turn(): pl.pallas_call(turn_kernel, grid=(n // t,), in_specs=[row, row, whole((d,...  87.9 us
    pallas_call x1, Pallas kernels, stepped(): pl.pallas_call(functools.partial(step_kernel, 4.0 * sum((w.size for w in...  15.8 us

profile of v1, /device:TPU:0, one launch (start us, length us, event | category | flops | bytes accessed | tf_op | source)
XLA Modules:
  0.0 394.9 jit_solution(17815142403949373933)
XLA Ops:
  0.6 99.6 %forward.1 = (bf16[4096,640]{1,0:T(8,128)(2,1)}, bf16[2,640,4096]{2,1,0:T(8,128)(2,1)}, f32[2,4,4096,512]{3,2,1,0:T(8,128)}, f32[2,4,4096,512]{3,2,1,0:T(8,128)}...) custom-call(bf16[4096,640]{1,0:T(8,128)(2,1)} %bitcast.3, ...), custom_call_target="tpu_custom_call" | custom-call | flops 32212254720 | bytes 100000000 | tf_op jit(solution)/shard_map/forward/pallas_call | solution.py:207
  100.3 87.9 %turn.1 = (bf16[2,4096,640]{2,1,0:T(8,128)(2,1)}, bf16[2,640,4096]{2,1,0:T(8,128)(2,1)}, bf16[2,640,4096]{2,1,0:T(8,128)(2,1)}, f32[2,4,4096,512]{3,2,1,0:T(8,128)}, f32[2,4,4096,512]{3,2,1,0:T(8,128)}) custom-call(bf16[4096,640]{1,0:T(8,128)(2,1)} %get-tuple-element.23.h_ref, ...), custom_call_target="tpu_custom_call", output_to_operand_aliasing={{2}: (5, {}), {3}: (6, {}), {4}: (7, {})} | custom-call | flops 53687091200 | bytes 100000000 | tf_op jit(solution)/shard_map/turn/pallas_call | solution.py:246
  188.1 190.7 %summed.1 = (bf16[8,2,4,240,128]{4,3,2,1,0:T(8,128)(2,1)}, f32[8,128]{1,0:T(8,128)}) custom-call(bf16[2,4096,640]{2,1,0:T(8,128)(2,1)} %get-tuple-element.30.dys_ref, bf16[2,640,4096]{2,1,0:T(8,128)(2,1)} %get-tuple-element.31.dyt_ref, bf16[2,640,4096]{2,1,0:T(8,128)(2,1)} %get-tuple-element.32.at_ref, f32[2,4,4096,512]{3,2,1,0:T(8,128)} %get-tuple-element.33.g_ref, ...), custom_call_target="tpu_custom_call" | custom-call | flops 85899345920 | bytes 200000000 | tf_op jit(solution)/shard_map/summed/pallas_call | solution.py:465
  378.9 15.8 %stepped.1 = (bf16[2,160,2048]{2,1,0:T(8,128)(2,1)}, bf16[2,160,2048]{2,1,0:T(8,128)(2,1)}, bf16[2,512,640]{2,1,0:T(8,128)(2,1)}, f32[2,160,2048]{2,1,0:T(8,128)...) custom-call(f32[8,128]{1,0:T(8,128)} %get-tuple-element.35.squares_r, ...), custom_call_target="tpu_custom_call" | custom-call | flops 30000000 | bytes 43000000 | tf_op jit(solution)/shard_map/stepped/pallas_call | solution.py:542

commit v2 on v1

--- a/solution.py
+++ b/solution.py
@@ -38,9 +38,9 @@
         ref[0, c, :, LANES * q : LANES * q + LANES] = value[:, LANES * c : LANES * c + LANES]
 
 
-def forward_kernel(x_ref, g_block, u_block, d_block, h_ref, at_ref, g_ref, u_ref, wg_all, wu_all, wd_all, z_ref, *scratch):
+def forward_kernel(x_ref, g_block, u_block, d_block, h_ref, at_ref, g_ref, u_ref, wg_all, wu_all, wd_all, a_all, acc, *scratch):
     own, held, sems_s, sems_r, sems_own, sems_held = scratch[:3], scratch[3:6], *scratch[6:]
-    step, steps = pl.program_id(0), pl.num_programs(0)
+    q, tile, tiles = pl.program_id(0), pl.program_id(1), pl.num_programs(1)
     rep, r, s = lax.axis_index("rep"), lax.axis_index("r"), lax.axis_index("s")
     ax, core, ay, az = s // 2, s % 2, r // 4, r % 4
     mate = (rep, r, ax * 2 + 1 - core)
@@ -49,67 +49,86 @@
     over = (rep, (1 - ay) * 4 + az, s)
     blocks, alls, halves = (g_block, u_block, d_block), (wg_all, wu_all, wd_all), (80, 80, 256)
 
-    def half(i, layer, place, which):
+    every = slice(None)
+    groups = [[(0, i, slice(WIDE * n, WIDE * n + WIDE)) for i in range(2)] for n in range(4)]
+    groups[0].append((0, 2, every))
+    groups.append([(1, i, every) for i in THREE])
+    order = [piece for group in groups for piece in group]
+
+    def rows(i, place, which=None):
         n = halves[i]
-        return alls[i].at[layer, pl.ds(pl.multiple_of(2 * n * place + n * which, 16), n)]
-
-    def copy(kind, i, layer, src, dst, who):
+        if which is None:
+            return pl.ds(pl.multiple_of(2 * n * place, 16), 2 * n)
+        return pl.ds(pl.multiple_of(2 * n * place + n * which, 16), n)
+
+    def copy(kind, piece, src, dst, who):
+        at = order.index(piece)
         return pltpu.make_async_remote_copy(
-            src_ref=src,
-            dst_ref=dst,
-            send_sem=sems_s.at[kind, layer, i],
-            recv_sem=sems_r.at[kind, layer, i],
-            device_id=who,
-            device_id_type=MESH,
+            src_ref=src, dst_ref=dst, send_sem=sems_s.at[kind, at], recv_sem=sems_r.at[kind, at], device_id=who, device_id_type=MESH
         )
 
-    def whole_block(i, layer, place):
-        n = 2 * halves[i]
-        return alls[i].at[layer, pl.ds(pl.multiple_of(n * place, 16), n)]
-
-    def to_mate(i, layer):
-        return copy(0, i, layer, blocks[i].at[layer], whole_block(i, layer, s), mate)
-
-    def to_across(i, layer):
-        n = halves[i]
-        return copy(1, i, layer, blocks[i].at[layer, pl.ds(pl.multiple_of(n * ay, 16), n)], half(i, layer, s, ay), across)
-
-    def to_over(i, layer):
-        return copy(2, i, layer, half(i, layer, far, ay), half(i, layer, far, ay), over)
-
-    def near_on(i, layer):
-        return copy(3, i, layer, half(i, layer, far, ay), half(i, layer, far, ay), mate)
-
-    def far_on(i, layer):
-        return copy(4, i, layer, half(i, layer, far, 1 - ay), half(i, layer, far, 1 - ay), mate)
+    def there(piece, *place):
+        layer, i, cols = piece
+        return alls[i].at[layer, rows(i, *place), cols]
+
+    def to_mate(piece):
+        layer, i, cols = piece
+        return copy(0, piece, blocks[i].at[layer, :, cols], there(piece, s), mate)
+
+    def to_across(piece):
+        layer, i, cols = piece
+        return copy(1, piece, blocks[i].at[layer, rows(i, 0, ay), cols], there(piece, s, ay), across)
+
+    def to_over(piece):
+        return copy(2, piece, there(piece, far, ay), there(piece, far, ay), over)
+
+    def near_on(piece):
+        return copy(3, piece, there(piece, far, ay), there(piece, far, ay), mate)
+
+    def far_on(piece):
+        return copy(4, piece, there(piece, far, 1 - ay), there(piece, far, 1 - ay), mate)
 
     def own_in(i, layer):
         return pltpu.make_async_copy(blocks[i].at[layer], own[i].at[layer], sems_own.at[0, layer, i])
 
     def own_out(i, layer):
-        return pltpu.make_async_copy(own[i].at[layer], whole_block(i, layer, s), sems_own.at[1, layer, i])
-
-    def first_half(layer):
-        for i in THREE:
-            to_across(i, layer).wait_recv()
-            to_over(i, layer).start()
-            near_on(i, layer).start()
-
-    def second_half(layer):
-        for i in THREE:
-            to_over(i, layer).wait_recv()
-            far_on(i, layer).start()
-
-    def finish(layer):
-        for i in THREE:
-            to_across(i, layer).wait_send()
-            to_over(i, layer).wait_send()
-            to_mate(i, layer).wait()
-            near_on(i, layer).wait()
-            far_on(i, layer).wait()
-            own_out(i, layer).wait()
-
-    @pl.when(step == 0)
+        return pltpu.make_async_copy(own[i].at[layer], alls[i].at[layer, rows(i, s)], sems_own.at[1, layer, i])
+
+    def send(group):
+        for piece in group:
+            to_across(piece).start()
+        for piece in group:
+            to_mate(piece).start()
+
+    def first_half(group):
+        for piece in group:
+            to_across(piece).wait_recv()
+            to_over(piece).start()
+            near_on(piece).start()
+
+    def second_half(group):
+        for piece in group:
+            to_over(piece).wait_recv()
+            far_on(piece).start()
+
+    def finish(group):
+        for piece in group:
+            to_across(piece).wait_send()
+            to_over(piece).wait_send()
+            to_mate(piece).wait()
+            near_on(piece).wait()
+            far_on(piece).wait()
+
+    def loads(n):
+        return [
+            pltpu.make_async_copy(alls[i].at[layer, :, cols], held[i] if i == 2 else held[i].at[n], sems_held.at[i, n])
+            for layer, i, cols in groups[n]
+        ]
+
+    def when(n, t):
+        return pl.when((q == n) & (tile == t))
+
+    @when(0, 0)
     def _():
         for layer in range(2):
             for i in THREE:
@@ -118,49 +137,89 @@
         for who in (mate, across, over):
             pl.semaphore_signal(barrier, inc=1, device_id=who, device_id_type=MESH)
         pl.semaphore_wait(barrier, 3)
+        send(groups[0])
         for layer in range(2):
             for i in THREE:
-                to_across(i, layer).start()
+                own_in(i, layer).wait()
+                own_out(i, layer).start()
+        first_half(groups[0])
+        for n in STEPS_Z:
+            send(groups[n])
+        second_half(groups[0])
+        finish(groups[0])
         for layer in range(2):
             for i in THREE:
-                to_mate(i, layer).start()
-                own_in(i, layer).wait()
-                own_out(i, layer).start()
-        first_half(0)
-        second_half(0)
-        finish(0)
-        loads = [pltpu.make_async_copy(alls[i].at[0], held[i], sems_held.at[i]) for i in THREE]
-        for load in loads:
+                own_out(i, layer).wait()
+        for load in loads(0):
             load.start()
-        for load in loads:
+        for load in loads(0):
             load.wait()
 
-    @pl.when(step == 1)
-    def _():
-        first_half(1)
-
-    @pl.when(step == 3)
-    def _():
-        second_half(1)
-
-    @pl.when(step == steps - 1)
-    def _():
-        finish(1)
+    @when(0, 1)
+    def _():
+        for n in STEPS_Z:
+            first_half(groups[n])
+        send(groups[4])
+
+    for n in STEPS_Z:
+
+        @when((n + 1) // 4, (n + 1) % 4)
+        def _():
+            second_half(groups[n])
+
+    for n in STEPS_Z:
+
+        @when(n - 1, 3)
+        def _():
+            finish(groups[n])
+            for load in loads(n):
+                load.start()
+
+        @when(n, 0)
+        def _():
+            for load in loads(n):
+                load.wait()
+
+    @when(2, 0)
+    def _():
+        first_half(groups[4])
+
+    @when(3, 2)
+    def _():
+        second_half(groups[4])
+
+    @when(3, 3)
+    def _():
+        finish(groups[4])
 
     wg_ref, wu_ref, wd_ref = held
-    x = x_ref[...]
-    wide = x.astype(F32)
-    a = (wide * scale_of(wide)).astype(BF16)
-    at_ref[0] = a.T
-    for q in range(4):
-        cols = slice(WIDE * q, WIDE * q + WIDE)
-        gate = dot(a, wg_ref[:, cols])
-        up = dot(a, wu_ref[:, cols])
-        keep(g_ref, gate, q)
-        keep(u_ref, up, q)
-        z_ref[:, cols] = (gate * sigmoid(gate) * up).astype(BF16)
-    out = dot(z_ref[...], wd_ref[...]).astype(BF16)
-    h_ref[...] = (wide + out.astype(F32)).astype(BF16)
+    n = x_ref.shape[0]
+    here = pl.ds(pl.multiple_of(n * tile, n), n)
+
+    @pl.when(q == 0)
+    def _():
+        wide = x_ref[...].astype(F32)
+        a = (wide * scale_of(wide)).astype(BF16)
+        a_all[here] = a
+        at_ref[0] = a.T
+        acc[here] = jnp.zeros_like(wide)
+
+    for part in range(2):
+        own_rows = pl.ds(pl.multiple_of(n * tile + n // 2 * part, n // 2), n // 2)
+        some = slice(n // 2 * part, n // 2 * part + n // 2)
+        a = a_all[own_rows]
+        gate = dot(a, wg_ref[q])
+        up = dot(a, wu_ref[q])
+        for c in range(4):
+            cols = slice(LANES * c, LANES * c + LANES)
+            g_ref[0, c, some] = gate[:, cols]
+            u_ref[0, c, some] = up[:, cols]
+        z = (gate * sigmoid(gate) * up).astype(BF16)
+        acc[own_rows] += dot(z, wd_ref[pl.ds(pl.multiple_of(WIDE * q, WIDE), WIDE)])
+
+    @pl.when(q == 3)
+    def _():
+        h_ref[...] = (x_ref[...].astype(F32) + acc[here].astype(BF16).astype(F32)).astype(BF16)
 
 
 def grads(gate, up, dz):
@@ -200,15 +259,23 @@
 def forward(x, wg, wu, wd):
     n, d = x.shape
     f = wg.shape[2]
-    t = TOKENS_F
-    row = pl.BlockSpec((t, d), lambda i: (i, 0))
-    kept = pl.BlockSpec((1, 4, t, f // 4), lambda i: (0, 0, i, 0))
+    t = TOKENS_B
+    row = pl.BlockSpec((t, d), lambda q, i: (i, 0))
+    kept = pl.BlockSpec((1, 4, t, LANES), lambda q, i: (0, 0, i, q))
     hbm = pl.BlockSpec(memory_space=pl.ANY)
     return pl.pallas_call(
         forward_kernel,
-        grid=(n // t,),
+        grid=(4, n // t),
         in_specs=[row, hbm, hbm, hbm],
-        out_specs=[row, pl.BlockSpec((1, d, t), lambda i: (0, 0, i)), kept, kept, hbm, hbm, hbm],
+        out_specs=[
+            pl.BlockSpec((t, d), lambda q, i: (jnp.where(q == 3, i, 0), 0)),
+            pl.BlockSpec((1, d, t), lambda q, i: (0, 0, jnp.where(q == 0, i, n // t - 1))),
+            kept,
+            kept,
+            hbm,
+            hbm,
+            hbm,
+        ],
         out_shape=[
             jax.ShapeDtypeStruct((n, d), BF16),
             jax.ShapeDtypeStruct((2, d, n), BF16),
@@ -219,15 +286,15 @@
             jax.ShapeDtypeStruct((2, f, d), BF16),
         ],
         scratch_shapes=[
-            pltpu.VMEM((t, f), BF16),
+            pltpu.VMEM((n, d), BF16),
+            pltpu.VMEM((n, d), F32),
             *[pltpu.VMEM(w.shape, BF16) for w in (wg, wu, wd)],
-            pltpu.VMEM((d, f), BF16),
-            pltpu.VMEM((d, f), BF16),
+            *[pltpu.VMEM((4, d, WIDE), BF16)] * 2,
             pltpu.VMEM((f, d), BF16),
-            pltpu.SemaphoreType.DMA((5, 2, 3)),
-            pltpu.SemaphoreType.DMA((5, 2, 3)),
+            pltpu.SemaphoreType.DMA((5, 12)),
+            pltpu.SemaphoreType.DMA((5, 12)),
             pltpu.SemaphoreType.DMA((2, 2, 3)),
-            pltpu.SemaphoreType.DMA((3,)),
+            pltpu.SemaphoreType.DMA((3, 4)),
         ],
         compiler_params=pltpu.CompilerParams(vmem_limit_bytes=LIMIT, collective_id=0, has_side_effects=True),
         cost_estimate=pl.CostEstimate(flops=6 * n * d * f, bytes_accessed=100_000_000, transcendentals=0),
@@ -301,8 +368,9 @@
     def by_core(j):
         return copy(p.at[j % 2, 1 - core], rc.at[j], 0, j, mate)
 
-    def by_x(j):
-        return copy(q.at[j % 2, 1 - x], rx.at[j], 1, j, across)
+    def by_x(j, kept):
+        which = y if kept else 1 - y
+        return copy(q.at[j % 2, 1 - x, which], rx.at[j, which], 10 if kept else 1, j, across)
 
     def by_y(j):
         return copy(sy.at[j % 2, 1 - y], ry.at[j], 2, j, over)
@@ -330,29 +398,39 @@
     def give(j):
         return pltpu.make_async_copy(fin.at[j], out_ref.at[j], fin_s.at[j])
 
+    def join_x(j, kept):
+        which = y if kept else 1 - y
+        by_x(j, kept).wait()
+        total = (q[j % 2, x, which].astype(F32) + rx[j, which].astype(F32)).astype(BF16)
+        for i in range(4):
+            sy[j % 2, which, i] = total[:, LANES * i : LANES * i + LANES]
+
     def at(rounds, when, j_ok=True):
         j = chunk - rounds
         return j, (part == when) & (j >= 0) & (j < CHUNKS)
 
-    j, now = at(1, 0)
+    j, now = at(1, 1)
 
     @pl.when(now)
     def _():
         by_core(j).wait()
         for k in range(2):
-            q[j % 2, k] = (p[j % 2, core, k].astype(F32) + rc[j, k].astype(F32)).astype(BF16)
-        by_x(j).start()
+            q[j % 2, k] = (p[j % 2, core, k].astype(F32) + rc[j, k].astype(F32)).astype(BF16).reshape(2, HALF, WIDE)
+        by_x(j, False).start()
+        by_x(j, True).start()
 
     j, now = at(2, 0)
 
     @pl.when(now)
     def _():
-        by_x(j).wait()
-        total = (q[j % 2, x].astype(F32) + rx[j].astype(F32)).astype(BF16)
-        for k in range(2):
-            for i in range(4):
-                sy[j % 2, k, i] = total[HALF * k : HALF * k + HALF, LANES * i : LANES * i + LANES]
+        join_x(j, False)
         by_y(j).start()
+
+    j, now = at(2, 1)
+
+    @pl.when(now)
+    def _():
+        join_x(j, True)
 
     j, now = at(2, 2)
 
@@ -479,14 +557,14 @@
             pltpu.VMEM((3, d, WIDE), F32),
             pltpu.VMEM((2, 2, 2, 480, WIDE), BF16),
             pltpu.VMEM((CHUNKS, 2, 480, WIDE), BF16),
-            pltpu.VMEM((2, 2, 480, WIDE), BF16),
-            pltpu.VMEM((CHUNKS, 480, WIDE), BF16),
+            pltpu.VMEM((2, 2, 2, HALF, WIDE), BF16),
+            pltpu.VMEM((CHUNKS, 2, HALF, WIDE), BF16),
             pltpu.VMEM((2, 2, 4, HALF, LANES), BF16),
             pltpu.VMEM((CHUNKS, 4, HALF, LANES), BF16),
             pltpu.VMEM((2, 4, HALF, LANES), BF16),
             pltpu.VMEM((CHUNKS, 3, HALF, LANES), BF16),
-            pltpu.SemaphoreType.DMA((10, CHUNKS)),
-            pltpu.SemaphoreType.DMA((10, CHUNKS)),
+            pltpu.SemaphoreType.DMA((11, CHUNKS)),
+            pltpu.SemaphoreType.DMA((11, CHUNKS)),
             *[pltpu.VMEM((TOKENS_B, WIDE), BF16)] * 3,
             pltpu.VMEM((4, 8, LANES), F32),
             pltpu.VMEM((3, 8, LANES), F32),

time: 395 us -> 368 us (0.932)
  Pallas kernels: 394 us -> 366 us
    pallas_call x1, Pallas kernels: 191 us -> 172 us  [summed(): pl.pallas_call(sum_kernel, grid=(steps,), in_specs=[spec((1, t, d), lambd...]
    pallas_call x1, Pallas kernels: 99.6 us -> 90.9 us  [forward(): pl.pallas_call(forward_kernel, grid=(4, n // t), in_specs=[row, hbm, hbm,...]
where the time goes in v2:
time: 368 us; the launch traced here: 367 us
  Pallas kernels  366 us (99%)
    pallas_call x1, Pallas kernels, summed(): pl.pallas_call(sum_kernel, grid=(steps,), in_specs=[spec((1, t, d), lambd...  172 us
    pallas_call x1, Pallas kernels, forward(): pl.pallas_call(forward_kernel, grid=(4, n // t), in_specs=[row, hbm, hbm,...  90.9 us
    pallas_call x1, Pallas kernels, turn(): pl.pallas_call(turn_kernel, grid=(n // t,), in_specs=[row, row, whole((d,...  87.8 us
    pallas_call x1, Pallas kernels, stepped(): pl.pallas_call(functools.partial(step_kernel, 4.0 * sum((w.size for w in...  15.8 us

profile of v2, /device:TPU:0, one launch (start us, length us, event | category | flops | bytes accessed | tf_op | source)
XLA Modules:
  0.0 367.3 jit_solution(14675057012399936741)
XLA Ops:
  0.6 90.9 %forward.1 = (bf16[4096,640]{1,0:T(8,128)(2,1)}, bf16[2,640,4096]{2,1,0:T(8,128)(2,1)}, f32[2,4,4096,512]{3,2,1,0:T(8,128)}, f32[2,4,4096,512]{3,2,1,0:T(8,128)}...) custom-call(bf16[4096,640]{1,0:T(8,128)(2,1)} %bitcast.3, ...), custom_call_target="tpu_custom_call" | custom-call | flops 32212254720 | bytes 100000000 | tf_op jit(solution)/shard_map/forward/pallas_call | solution.py:266
  91.6 87.8 %turn.1 = (bf16[2,4096,640]{2,1,0:T(8,128)(2,1)}, bf16[2,640,4096]{2,1,0:T(8,128)(2,1)}, bf16[2,640,4096]{2,1,0:T(8,128)(2,1)}, f32[2,4,4096,512]{3,2,1,0:T(8,128)}, f32[2,4,4096,512]{3,2,1,0:T(8,128)}) custom-call(bf16[4096,640]{1,0:T(8,128)(2,1)} %get-tuple-element.23.h_ref, ...), custom_call_target="tpu_custom_call", output_to_operand_aliasing={{2}: (5, {}), {3}: (6, {}), {4}: (7, {})} | custom-call | flops 53687091200 | bytes 100000000 | tf_op jit(solution)/shard_map/turn/pallas_call | solution.py:313
  179.4 171.9 %summed.1 = (bf16[8,2,4,240,128]{4,3,2,1,0:T(8,128)(2,1)}, f32[8,128]{1,0:T(8,128)}) custom-call(bf16[2,4096,640]{2,1,0:T(8,128)(2,1)} %get-tuple-element.30.dys_ref, bf16[2,640,4096]{2,1,0:T(8,128)(2,1)} %get-tuple-element.31.dyt_ref, bf16[2,640,4096]{2,1,0:T(8,128)(2,1)} %get-tuple-element.32.at_ref, f32[2,4,4096,512]{3,2,1,0:T(8,128)} %get-tuple-element.33.g_ref, ...), custom_call_target="tpu_custom_call" | custom-call | flops 85899345920 | bytes 200000000 | tf_op jit(solution)/shard_map/summed/pallas_call | solution.py:543
  351.3 15.8 %stepped.1 = (bf16[2,160,2048]{2,1,0:T(8,128)(2,1)}, bf16[2,160,2048]{2,1,0:T(8,128)(2,1)}, bf16[2,512,640]{2,1,0:T(8,128)(2,1)}, f32[2,160,2048]{2,1,0:T(8,128)...) custom-call(f32[8,128]{1,0:T(8,128)} %get-tuple-element.35.squares_r, ...), custom_call_target="tpu_custom_call" | custom-call | flops 30000000 | bytes 43000000 | tf_op jit(solution)/shard_map/stepped/pallas_call | solution.py:620
